TPU v7x, 16 devices: a whole 2x2x2 slice. The times are simulated.
16 devices in a mesh: ep: 4 (over z, y), dp: 4 (over x, core).
Axes of the slice: x: 2, y: 2, z: 2, core: 2. Of those that a mesh axis runs over, the one named last changes fastest.
Arguments:
- act_in: bfloat16 [16384, 512], P(('ep', 'dp'))
- grad_out: bfloat16 [16384, 512], P(('ep', 'dp'))
- slot_ids: int32 [2, 16384, 6], P(None, ('ep', 'dp'))
- gate_vals: float32 [2, 16384, 6], P(None, ('ep', 'dp'))
- w_dense: bfloat16 [2, 512, 512], replicated
- w_gate: bfloat16 [2, 64, 512, 352], P(None, 'ep')
- w_up: bfloat16 [2, 64, 512, 352], P(None, 'ep')
- w_down: bfloat16 [2, 64, 352, 512], P(None, 'ep')
- ws_gate: bfloat16 [2, 512, 704], replicated
- ws_up: bfloat16 [2, 512, 704], replicated
- ws_down: bfloat16 [2, 704, 512], replicated
Outputs:
- output 1: bfloat16 [16384, 512], P(('ep', 'dp'))
- output 2: bfloat16 [2, 512, 512], replicated
- output 3: bfloat16 [2, 64, 512, 352], P(None, 'ep')
- output 4: bfloat16 [2, 64, 512, 352], P(None, 'ep')
- output 5: bfloat16 [2, 64, 352, 512], P(None, 'ep')
- output 6: bfloat16 [2, 512, 704], replicated
- output 7: bfloat16 [2, 512, 704], replicated
- output 8: bfloat16 [2, 704, 512], replicated
All inputs are finite; a program needn't handle non-finite values.
Results may differ from a plain program's by a relative error of at most 0.02.
Values are sent between devices in bfloat16 or wider.
A program may use at most 1 GiB of HBM per device.

v0:
```python
import jax
import jax.numpy as jnp
from jax import lax
from jax.sharding import PartitionSpec as P

ALL_AXES = ("ep", "dp")


def silu_grad(pre_act):
    sigma = jax.nn.sigmoid(pre_act)
    return sigma * (1.0 + pre_act * (1.0 - sigma))


def contract_rows(left, right):
    return lax.dot_general(left, right, (((0,), (0,)), ((), ())), preferred_element_type=jnp.float32)


def contract_cols(left, right):
    return lax.dot_general(left, right, (((1,), (1,)), ((), ())), preferred_element_type=jnp.float32)


def layer_front(act, weights, slot_ids, ep_size):
    w_dense, w_gate, w_up, w_down, ws_gate, ws_up, ws_down = weights
    tokens, width = act.shape
    top = slot_ids.shape[1]
    local_exp = w_gate.shape[0]
    capacity = 2 * tokens * top // (local_exp * ep_size)
    dense_pre = jnp.dot(act, w_dense, preferred_element_type=jnp.float32)
    mixed = (act.astype(jnp.float32) + dense_pre).astype(jnp.bfloat16)
    slot_flat = slot_ids.reshape(tokens * top)
    copy_ids = jnp.arange(1, tokens * top + 1, dtype=jnp.int32)
    slot_owner = jnp.zeros((local_exp * ep_size * capacity,), jnp.int32).at[slot_flat].set(copy_ids)
    tok_owner = (slot_owner + top - 1) // top
    mixed_ext = jnp.concatenate([jnp.zeros((1, width), mixed.dtype), mixed], axis=0)
    send_buf = jnp.take(mixed_ext, tok_owner, axis=0).reshape(ep_size, local_exp, capacity, width)
    recv_rows = lax.all_to_all(send_buf, "ep", 0, 1).reshape(local_exp, ep_size * capacity, width)
    a_one = jnp.einsum("erd,edf->erf", recv_rows, w_gate, preferred_element_type=jnp.float32)
    a_three = jnp.einsum("erd,edf->erf", recv_rows, w_up, preferred_element_type=jnp.float32)
    hidden = (jax.nn.silu(a_one) * a_three).astype(jnp.bfloat16)
    s_one = jnp.dot(mixed, ws_gate, preferred_element_type=jnp.float32)
    s_three = jnp.dot(mixed, ws_up, preferred_element_type=jnp.float32)
    shared_hidden = (jax.nn.silu(s_one) * s_three).astype(jnp.bfloat16)
    return (act, mixed, slot_flat, slot_owner, recv_rows, a_one, a_three, hidden, s_one, s_three, shared_hidden)


def layer_finish(saved, weights, gate_vals, ep_size):
    act, mixed, slot_flat, slot_owner, recv_rows, a_one, a_three, hidden, s_one, s_three, shared_hidden = saved
    w_down = weights[3]
    ws_down = weights[6]
    tokens, width = mixed.shape
    top = gate_vals.shape[1]
    local_exp = hidden.shape[0]
    capacity = recv_rows.shape[1] // ep_size
    exp_out = jnp.einsum("erf,efd->erd", hidden, w_down, preferred_element_type=jnp.float32).astype(jnp.bfloat16)
    back_rows = lax.all_to_all(exp_out.reshape(local_exp, ep_size, capacity, width), "ep", 1, 0).reshape(local_exp * ep_size * capacity, width)
    picked = jnp.take(back_rows, slot_flat, axis=0).reshape(tokens, top, width)
    routed = jnp.sum(gate_vals[:, :, None] * picked.astype(jnp.float32), axis=1)
    shared_out = jnp.dot(shared_hidden, ws_down, preferred_element_type=jnp.float32)
    return (mixed.astype(jnp.float32) + routed + shared_out).astype(jnp.bfloat16)


def layer_backward(grad_y, saved, weights, gate_vals, ep_size):
    act, mixed, slot_flat, slot_owner, recv_rows, a_one, a_three, hidden, s_one, s_three, shared_hidden = saved
    w_dense, w_gate, w_up, w_down, ws_gate, ws_up, ws_down = weights
    tokens, width = grad_y.shape
    top = gate_vals.shape[1]
    local_exp = hidden.shape[0]
    capacity = recv_rows.shape[1] // ep_size
    grad_y32 = grad_y.astype(jnp.float32)
    grad_pick = (gate_vals[:, :, None] * grad_y32[:, None, :]).astype(jnp.bfloat16).reshape(tokens * top, width)
    grad_ext = jnp.concatenate([jnp.zeros((1, width), grad_pick.dtype), grad_pick], axis=0)
    send_grad = jnp.take(grad_ext, slot_owner, axis=0).reshape(ep_size, local_exp, capacity, width)
    grad_exp_out = lax.all_to_all(send_grad, "ep", 0, 1).reshape(local_exp, ep_size * capacity, width)
    g_w_down = jnp.einsum("erf,erd->efd", hidden, grad_exp_out, preferred_element_type=jnp.float32)
    grad_hidden = jnp.einsum("erd,efd->erf", grad_exp_out, w_down, preferred_element_type=jnp.float32)
    grad_a_one = (grad_hidden * a_three * silu_grad(a_one)).astype(jnp.bfloat16)
    grad_a_three = (grad_hidden * jax.nn.silu(a_one)).astype(jnp.bfloat16)
    g_w_gate = jnp.einsum("erd,erf->edf", recv_rows, grad_a_one, preferred_element_type=jnp.float32)
    g_w_up = jnp.einsum("erd,erf->edf", recv_rows, grad_a_three, preferred_element_type=jnp.float32)
    grad_rows = (jnp.einsum("erf,edf->erd", grad_a_one, w_gate, preferred_element_type=jnp.float32) + jnp.einsum("erf,edf->erd", grad_a_three, w_up, preferred_element_type=jnp.float32)).astype(jnp.bfloat16)
    grad_back = lax.all_to_all(grad_rows.reshape(local_exp, ep_size, capacity, width), "ep", 1, 0).reshape(local_exp * ep_size * capacity, width)
    grad_routed = jnp.sum(jnp.take(grad_back, slot_flat, axis=0).reshape(tokens, top, width).astype(jnp.float32), axis=1)
    g_ws_down = contract_rows(shared_hidden, grad_y)
    grad_shared = contract_cols(grad_y, ws_down)
    grad_s_one = (grad_shared * s_three * silu_grad(s_one)).astype(jnp.bfloat16)
    grad_s_three = (grad_shared * jax.nn.silu(s_one)).astype(jnp.bfloat16)
    g_ws_gate = contract_rows(mixed, grad_s_one)
    g_ws_up = contract_rows(mixed, grad_s_three)
    grad_mixed = (grad_y32 + grad_routed + contract_cols(grad_s_one, ws_gate) + contract_cols(grad_s_three, ws_up)).astype(jnp.bfloat16)
    g_w_dense = contract_rows(act, grad_mixed)
    grad_act = (grad_mixed.astype(jnp.float32) + contract_cols(grad_mixed, w_dense)).astype(jnp.bfloat16)
    dense_grads = (g_w_dense.astype(jnp.bfloat16), g_ws_gate.astype(jnp.bfloat16), g_ws_up.astype(jnp.bfloat16), g_ws_down.astype(jnp.bfloat16))
    expert_grads = (g_w_gate.astype(jnp.bfloat16), g_w_up.astype(jnp.bfloat16), g_w_down.astype(jnp.bfloat16))
    return grad_act, dense_grads, expert_grads


def solution(mesh):
    ep_size = mesh.shape["ep"]
    tok_spec = P(ALL_AXES, None)
    route_spec = P(None, ALL_AXES, None)
    exp_spec = P(None, "ep", None, None)
    repl_spec = P(None, None, None)

    def body(act_in, grad_out, slot_ids, gate_vals, w_dense, w_gate, w_up, w_down, ws_gate, ws_up, ws_down):
        layers = w_dense.shape[0]
        all_weights = [(w_dense[layer], w_gate[layer], w_up[layer], w_down[layer], ws_gate[layer], ws_up[layer], ws_down[layer]) for layer in range(layers)]
        saved_all = []
        act = act_in
        for layer in range(layers):
            saved = layer_front(act, all_weights[layer], slot_ids[layer], ep_size)
            saved_all.append(saved)
            if layer + 1 < layers:
                act = layer_finish(saved, all_weights[layer], gate_vals[layer], ep_size)
        grad_act = grad_out
        dense_sums = [None] * layers
        expert_sums = [None] * layers
        for layer in reversed(range(layers)):
            grad_act, dense_grads, expert_grads = layer_backward(grad_act, saved_all[layer], all_weights[layer], gate_vals[layer], ep_size)
            dense_sums[layer] = [lax.psum(part, ALL_AXES) for part in dense_grads]
            expert_sums[layer] = [lax.psum(part, "dp") for part in expert_grads]
        dense_out = [jnp.stack([dense_sums[layer][which] for layer in range(layers)]) for which in range(4)]
        expert_out = [jnp.stack([expert_sums[layer][which] for layer in range(layers)]) for which in range(3)]
        return (grad_act, dense_out[0], expert_out[0], expert_out[1], expert_out[2], dense_out[1], dense_out[2], dense_out[3])

    return jax.shard_map(body, mesh=mesh, in_specs=(tok_spec, tok_spec, route_spec, route_spec, repl_spec, exp_spec, exp_spec, exp_spec, repl_spec, repl_spec, repl_spec), out_specs=(tok_spec, repl_spec, exp_spec, exp_spec, exp_spec, repl_spec, repl_spec, repl_spec), check_vma=False)
```

profile of v0, /device:TPU:0, one launch (start us, length us, event | category | flops | bytes accessed | tf_op | source)
XLA Modules:
  0.0 2285.7 jit_solution(4872411742493708446)
XLA Ops:
  8.8 23.0 %scatter_custom_fusion.1 = s32[12288]{0:T(1024)S(1)} fusion(s32[6144]{0:T(1024)S(1)} %bitcast.238, s32[6144]{0:T(1024)S(1)} %iota_add_fusion, s32[]{:T(128)} %constant.48.clone.1), kind=kCustom, calls=%fused_computation.175 | custom fusion | bytes 49156 | tf_op jit(solution)/shard_map/scatter | solution.py:32
  36.7 50.1 %gather_fusion.1 = bf16[12288,512]{1,0:T(8,128)(2,1)} fusion(bf16[1025,512]{1,0:T(8,128)(2,1)S(1)} %concatenate.13, s32[12288]{0:T(1024)S(1)} %get-tuple-element.60), kind=kCustom, calls=%fused_computation.1.clone | custom fusion | bytes 25214976 | tf_op jit(solution)/shard_map/jit(_take)/gather | solution.py:35
  93.6 143.4 %all_to_all.105 = bf16[4,16,1,192,512]{4,3,1,2,0:T(8,128)(2,1)S(1)} all-to-all(bf16[4,16,1,192,512]{4,3,1,2,0:T(8,128)(2,1)S(1)} %bitcast.229), channel_id=1, replica_groups=mesh['ep'=4,'dp'=4] {'ep'}, dimensions={0} | all-to-all | bytes 25165824 | tf_op jit(solution)/shard_map/all_to_all | solution.py:36
  256.7 23.2 %multiply_convert_fusion.5 = (bf16[16,768,352]{1,2,0:T(8,128)(2,1)}, f32[16,768,352]{1,2,0:T(8,128)}) fusion(f32[16,768,352]{1,2,0:T(8,128)} %fusion.20, bf16[16,768,512]{2,1,0:T(8,128)(2,1)} %bitcast.221, bf16[2,16,512,352]{2,3,1,0:T(8,128)(2,1)} %param.23), kind=kOutput, calls=%fused_computation.18 | convolution fusion | flops 4455137280 | bytes 61603840 | tf_op jit(solution)/shard_map/erd,edf->erf/dot_general | solution.py:38
  311.3 23.5 %scatter_custom_fusion = s32[12288]{0:T(1024)S(1)} fusion(s32[6144]{0:T(1024)S(1)} %bitcast.237, s32[6144]{0:T(1024)S(1)} %iota_add_fusion, s32[]{:T(128)} %constant.48.clone.1), kind=kCustom, calls=%fused_computation.177 | custom fusion | bytes 49156 | tf_op jit(solution)/shard_map/scatter | solution.py:32
  368.7 54.0 %gather_fusion = bf16[12288,512]{1,0:T(8,128)(2,1)} fusion(bf16[6145,512]{1,0:T(8,128)(2,1)} %concatenate.12, s32[12288]{0:T(1024)S(1)} %get-tuple-element.63), kind=kCustom, calls=%fused_computation.clone | custom fusion | bytes 25214976 | tf_op jit(solution)/shard_map/jit(_take)/gather | solution.py:72
  459.3 31.9 %gather_fusion.2 = bf16[6144,512]{1,0:T(8,128)(2,1)} fusion(bf16[12288,512]{1,0:T(8,128)(2,1)} %bitcast.21, s32[6144]{0:T(1024)S(1)} %fusion.99), kind=kCustom, calls=%fused_computation.2.clone | custom fusion | bytes 12607488 | tf_op jit(solution)/shard_map/jit(_take)/gather | solution.py:56
  526.5 50.1 %gather_fusion.3 = bf16[12288,512]{1,0:T(8,128)(2,1)} fusion(bf16[1025,512]{1,0:T(8,128)(2,1)S(1)} %concatenate.14, s32[12288]{0:T(1024)S(1)} %get-tuple-element.64), kind=kCustom, calls=%fused_computation.4.clone | custom fusion | bytes 25214976 | tf_op jit(solution)/shard_map/jit(_take)/gather | solution.py:35
  607.0 125.8 %all-to-all-done.3 = bf16[4,16,1,192,512]{4,3,1,2,0:T(8,128)(2,1)} async-done(((bf16[4,16,1,192,512]{4,3,1,2,0:T(8,128)(2,1)}), bf16[4,16,1,192,512]{4,3,1,2,0:T(8,128)(2,1)}, u32[]{:S(2)}, u32[]{:S(2)}) %all-to-all-start.3) | async-done | bytes 12582944 | tf_op jit(solution)/shard_map/all_to_all | solution.py:36
  772.2 24.3 %multiply_convert_fusion.3 = (bf16[16,768,352]{1,2,0:T(8,128)(2,1)}, bf16[16,768,352]{1,2,0:T(8,128)(2,1)}) fusion(f32[16,768,352]{1,2,0:T(8,128)} %fusion.5, f32[16,768,352]{1,2,0:T(8,128)} %fusion.9, bf16[16,768,512]{2,1,0:T(8,128)(2,1)} %bitcast.231, bf16[2,16,352,512]{3,2,1,0:T(8,128)(2,1)} %param.24), kind=kOutput, calls=%fused_computation.14 | convolution fusion | flops 4485414912 | bytes 70254592 | tf_op jit(solution)/shard_map/erd,efd->erf/dot_general | solution.py:75
  796.5 15.8 fusion.3
  812.3 20.3 add_convert_fusion.1
  863.3 123.4 %all-to-all-done.4 = bf16[1,16,4,192,512]{4,3,1,0,2:T(8,128)(2,1)} async-done(((bf16[1,16,4,192,512]{4,3,1,0,2:T(8,128)(2,1)}), bf16[1,16,4,192,512]{4,3,1,0,2:T(8,128)(2,1)}, u32[]{:S(2)}, u32[]{:S(2)}) %all-to-all-start.4) | async-done | bytes 12582944 | tf_op jit(solution)/shard_map/all_to_all | solution.py:81
  986.7 31.9 %gather_fusion.4 = bf16[6144,512]{1,0:T(8,128)(2,1)} fusion(bf16[12288,512]{1,0:T(8,128)(2,1)} %bitcast.36, s32[6144]{0:T(1024)S(1)} %fusion.100), kind=kCustom, calls=%fused_computation.5.clone | custom fusion | bytes 12607488 | tf_op jit(solution)/shard_map/jit(_take)/gather | solution.py:82
  1089.1 54.0 %gather_fusion.5 = bf16[12288,512]{1,0:T(8,128)(2,1)} fusion(bf16[6145,512]{1,0:T(8,128)(2,1)} %concatenate.15, s32[12288]{0:T(1024)S(1)} %copy-done.41), kind=kCustom, calls=%fused_computation.3.clone | custom fusion | bytes 25214976 | tf_op jit(solution)/shard_map/jit(_take)/gather | solution.py:72
  1181.6 115.5 %all-to-all-done.5 = bf16[4,16,1,192,512]{4,3,1,2,0:T(8,128)(2,1)} async-done(((bf16[4,16,1,192,512]{4,3,1,2,0:T(8,128)(2,1)}), bf16[4,16,1,192,512]{4,3,1,2,0:T(8,128)(2,1)}, u32[]{:S(2)}, u32[]{:S(2)}) %all-to-all-start.5) | async-done | bytes 12582944 | tf_op jit(solution)/shard_map/all_to_all | solution.py:73
  1307.8 24.1 %multiply_convert_fusion.2 = (bf16[16,768,352]{1,2,0:T(8,128)(2,1)}, bf16[16,768,352]{1,2,0:T(8,128)(2,1)}) fusion(f32[16,768,352]{1,2,0:T(8,128)} %fusion.20, f32[16,768,352]{1,2,0:T(8,128)} %get-tuple-element.70, bf16[16,768,512]{2,1,0:T(8,128)(2,1)} %bitcast.233, bf16[2,16,352,512]{3,2,1,0:T(8,128)(2,1)} %param.24), kind=kOutput, calls=%fused_computation.13 | convolution fusion | flops 4485414912 | bytes 70254592 | tf_op jit(solution)/shard_map/erd,efd->erf/dot_general | solution.py:75
  1331.9 15.8 fusion.14
  1347.7 20.7 add_convert_fusion
  1399.6 21.5 convert_bitcast_fusion
  1446.5 75.3 %all-to-all-done.6 = bf16[1,16,4,192,512]{4,3,1,0,2:T(8,128)(2,1)} async-done(((bf16[1,16,4,192,512]{4,3,1,0,2:T(8,128)(2,1)}), bf16[1,16,4,192,512]{4,3,1,0,2:T(8,128)(2,1)}, u32[]{:S(2)}, u32[]{:S(2)}) %all-to-all-start.6) | async-done | bytes 12582944 | tf_op jit(solution)/shard_map/all_to_all | solution.py:81
  1521.8 31.9 %gather_fusion.6 = bf16[6144,512]{1,0:T(8,128)(2,1)} fusion(bf16[12288,512]{1,0:T(8,128)(2,1)} %bitcast.48, s32[6144]{0:T(1024)S(1)} %copy-done.40), kind=kCustom, calls=%fused_computation.6.clone | custom fusion | bytes 12607488 | tf_op jit(solution)/shard_map/jit(_take)/gather | solution.py:82
  1623.4 56.0 %all-reduce.9.cloned.1.call-done = (bf16[1,512,512]{1,2,0:T(8,128)(2,1)}, bf16[1,512,512]{1,2,0:T(8,128)(2,1)}, bf16[1,512,704]{1,2,0:T(8,128)(2,1)}, bf16[1,512...) async-done(((bf16[1,512,512]{1,2,0:T(8,128)(2,1)}, ...) | async-done | bytes 5373968 | tf_op jit(solution)/shard_map/psum | solution.py:119
  1687.7 567.6 %all-reduce.11.cloned.1.call-done = (bf16[1,16,512,352]{2,3,1,0:T(8,128)(2,1)}, bf16[1,16,512,352]{2,3,1,0:T(8,128)(2,1)}, bf16[1,16,512,352]{2,3,1,0:T(8,128)(2...) async-done(((bf16[1,16,512,352]{2,3,1,0:T(8,128)(2,1)}, bf16[1,16,512,352]{2,3,1,0:T(8,128)(2,1)}, ...) | async-done | bytes 34603024 | tf_op jit(solution)/shard_map/psum | solution.py:120
  (225 shorter events, 547.7 us)
Async XLA Ops:
  8.3 24.8 %copy-start.19 = (s32[1,1024,6]{2,1,0:T(8,128)}, s32[1,1024,6]{2,1,0:T(8,128)S(1)}, u32[]{:S(2)}) copy-start(s32[1,1024,6]{2,1,0:T(8,128)S(1)} %copy.53) | copy-start | bytes 73732
  304.1 30.7 %copy-start.46 = (f32[2,1024,6]{1,0,2:T(2,128)S(1)}, f32[2,1024,6]{1,0,2:T(2,128)}, u32[]{:S(2)}) copy-start(f32[2,1024,6]{1,0,2:T(2,128)} %param.20) | copy-start | bytes 147460
  304.1 31.3 %copy-start.21 = (bf16[1024,512]{1,0:T(8,128)(2,1)S(1)}, bf16[1024,512]{1,0:T(8,128)(2,1)}, u32[]{:S(2)}) copy-start(bf16[1024,512]{1,0:T(8,128)(2,1)} %param.18) | copy-start | bytes 3145732
  304.1 142.4 %all-to-all-start.2 = ((bf16[1,16,4,192,512]{4,3,1,0,2:T(8,128)(2,1)}), bf16[1,16,4,192,512]{4,3,1,0,2:T(8,128)(2,1)}, u32[]{:S(2)}, u32[]{:S(2)}) async-start(bf16[1,16,4,192,512]{4,3,1,0,2:T(8,128)(2,1)} %copy.57), calls=%async_computation.2 | async-start | bytes 25165824 | tf_op jit(solution)/shard_map/all_to_all | solution.py:55
  310.9 32.6 %copy-start.17 = (s32[1,1024,6]{2,1,0:T(8,128)}, s32[1,1024,6]{2,1,0:T(8,128)S(1)}, u32[]{:S(2)}) copy-start(s32[1,1024,6]{2,1,0:T(8,128)S(1)} %copy.46) | copy-start | bytes 73732
  446.6 143.2 %all-to-all-start = ((bf16[4,16,1,192,512]{4,3,1,2,0:T(8,128)(2,1)}), bf16[4,16,1,192,512]{4,3,1,2,0:T(8,128)(2,1)}, u32[]{:S(2)}, u32[]{:S(2)}) async-start(bf16[4,16,1,192,512]{4,3,1,2,0:T(8,128)(2,1)} %bitcast.226), calls=%async_computation | async-start | bytes 25165824 | tf_op jit(solution)/shard_map/all_to_all | solution.py:73
  453.9 59.9 %copy-start.15 = (f32[1,1024,6]{2,1,0:T(8,128)}, f32[1,1024,6]{2,1,0:T(8,128)S(1)}, u32[]{:S(2)}) copy-start(f32[1,1024,6]{2,1,0:T(8,128)S(1)} %copy.69) | copy-start | bytes 73732
  453.9 37.3 %copy-start.43 = (pred[6144]{0:T(1024)(128)(4,1)}, pred[6144]{0:T(1024)(128)(4,1)S(1)}, u32[]{:S(2)}) copy-start(pred[6144]{0:T(1024)(128)(4,1)S(1)} %compare_and_fusion.5) | copy-start | bytes 18436
  589.8 143.1 %all-to-all-start.3 = ((bf16[4,16,1,192,512]{4,3,1,2,0:T(8,128)(2,1)}), bf16[4,16,1,192,512]{4,3,1,2,0:T(8,128)(2,1)}, u32[]{:S(2)}, u32[]{:S(2)}) async-start(bf16[4,16,1,192,512]{4,3,1,2,0:T(8,128)(2,1)} %bitcast.228), calls=%async_computation.3 | async-start | bytes 25165824 | tf_op jit(solution)/shard_map/all_to_all | solution.py:36
  843.3 143.4 %all-to-all-start.4 = ((bf16[1,16,4,192,512]{4,3,1,0,2:T(8,128)(2,1)}), bf16[1,16,4,192,512]{4,3,1,0,2:T(8,128)(2,1)}, u32[]{:S(2)}, u32[]{:S(2)}) async-start(bf16[1,16,4,192,512]{4,3,1,0,2:T(8,128)(2,1)} %copy.60), calls=%async_computation.4 | async-start | bytes 25165824 | tf_op jit(solution)/shard_map/all_to_all | solution.py:81
  1063.8 15.6 copy-start.42
  1089.1 54.0 %copy-start.45 = (pred[12288]{0:T(1024)(128)(4,1)S(1)}, pred[12288]{0:T(1024)(128)(4,1)}, u32[]{:S(2)}) copy-start(pred[12288]{0:T(1024)(128)(4,1)} %get-tuple-element.57) | copy-start | bytes 36868
  1154.1 142.9 %all-to-all-start.5 = ((bf16[4,16,1,192,512]{4,3,1,2,0:T(8,128)(2,1)}), bf16[4,16,1,192,512]{4,3,1,2,0:T(8,128)(2,1)}, u32[]{:S(2)}, u32[]{:S(2)}) async-start(bf16[4,16,1,192,512]{4,3,1,2,0:T(8,128)(2,1)} %bitcast.227), calls=%async_computation.5 | async-start | bytes 25165824 | tf_op jit(solution)/shard_map/all_to_all | solution.py:73
  1379.1 142.8 %all-to-all-start.6 = ((bf16[1,16,4,192,512]{4,3,1,0,2:T(8,128)(2,1)}), bf16[1,16,4,192,512]{4,3,1,0,2:T(8,128)(2,1)}, u32[]{:S(2)}, u32[]{:S(2)}) async-start(bf16[1,16,4,192,512]{4,3,1,0,2:T(8,128)(2,1)} %copy.64), calls=%async_computation.6 | async-start | bytes 25165824 | tf_op jit(solution)/shard_map/all_to_all | solution.py:81
  1385.4 294.0 %all-reduce.9.cloned.1.call-start = ((), (), s32[]{:S(2)}) async-start(), calls=%async_computation.7 | async-start | bytes 10747904 | tf_op jit(solution)/shard_map/psum | solution.py:119
  1399.6 21.5 copy-start.33
  1399.6 21.5 copy-start.57
  1399.6 23.1 %copy-start.25 = (bf16[1024,512]{1,0:T(8,128)(2,1)S(1)}, bf16[1024,512]{1,0:T(8,128)(2,1)}, u32[]{:S(2)}) copy-start(bf16[1024,512]{1,0:T(8,128)(2,1)} %copy-done.24) | copy-start | bytes 3145732
  1399.6 23.1 %copy-start.55 = (bf16[1024,704]{0,1:T(8,128)(2,1)S(1)}, bf16[1024,704]{0,1:T(8,128)(2,1)}, u32[]{:S(2)}) copy-start(bf16[1024,704]{0,1:T(8,128)(2,1)} %get-tuple-element.71) | copy-start | bytes 4325380
  1432.3 89.5 %copy-start.40 = (s32[6144]{0:T(1024)S(1)}, s32[6144]{0:T(1024)}, u32[]{:S(2)}) copy-start(s32[6144]{0:T(1024)} %copy-done.39) | copy-start | bytes 73732
  1521.8 31.9 %copy-start.44 = (pred[6144]{0:T(1024)(128)(4,1)S(1)}, pred[6144]{0:T(1024)(128)(4,1)}, u32[]{:S(2)}) copy-start(pred[6144]{0:T(1024)(128)(4,1)} %copy-done.43) | copy-start | bytes 18436
  1591.6 663.6 %all-reduce.11.cloned.1.call-start = ((), (), s32[]{:S(2)}) async-start(), calls=%async_computation.8 | async-start | bytes 69206016 | tf_op jit(solution)/shard_map/psum | solution.py:120
  2255.3 13.6 copy-start.13
  2255.3 15.2 copy-start.14
  (45 other events, 198.2 us)
Sparse Core Ops, SparseCore 0:
  1591.8 87.5 all-reduce.8
  1683.0 572.2 all-reduce.10
where the time goes:
time: 2290 us
  waiting for transfers between devices  1080 us (47%)
  local copies, waits for them, and re-layouts  539 us (24%)
  matrix products  339 us (15%)
  blocking collectives  143 us (6%)
  other arithmetic  131 us (6%)
  starting transfers between devices  39.6 us (2%)
    psum x1, waiting for transfers between devices, body(): expert_sums[layer] = [lax.psum(part, 'dp') for part in expert_grads]  568 us
    all_to_all x2, waiting for transfers between devices, layer_backward(): lax.all_to_all(grad_rows.reshape(local_exp, ep_size, capacity, width), 'e...  199 us
    all_to_all x1, blocking collectives, layer_front(): lax.all_to_all(send_buf, 'ep', 0, 1)  143 us
    all_to_all x1, waiting for transfers between devices, layer_front(): lax.all_to_all(send_buf, 'ep', 0, 1)  126 us
    all_to_all x2, waiting for transfers between devices, layer_backward(): lax.all_to_all(send_grad, 'ep', 0, 1)  118 us
    gather x2, local copies, waits for them, and re-layouts, layer_backward(): jnp.take(grad_ext, slot_owner, axis=0)  108 us
    gather x2, local copies, waits for them, and re-layouts, layer_front(): jnp.take(mixed_ext, tok_owner, axis=0)  100 us
    gather x2, local copies, waits for them, and re-layouts, layer_backward(): jnp.take(grad_back, slot_flat, axis=0).reshape(tokens, top, width)  63.8 us
  transfers between devices with their start and end apart: 8, of which 8 were waited for; matrix products, arithmetic and copies ran while one was open for 17% of the time, Pallas kernels for 0%

commit v1 on v0

v1 whole, which is shorter than its diff:
```python
import functools

import jax
import jax.numpy as jnp
from jax import lax
from jax.experimental import pallas as pl
from jax.experimental.pallas import tpu as pltpu
from jax.sharding import PartitionSpec as P

ALL_AXES = ("ep", "dp")
BF = jnp.bfloat16
F32 = jnp.float32
VMEM_LIMIT = 60 * 1024 * 1024


def silu_grad(pre_act):
    sigma = jax.nn.sigmoid(pre_act)
    return sigma * (1.0 + pre_act * (1.0 - sigma))


def contract_rows(left, right):
    return lax.dot_general(left, right, (((0,), (0,)), ((), ())), preferred_element_type=F32)


def contract_cols(left, right):
    return lax.dot_general(left, right, (((1,), (1,)), ((), ())), preferred_element_type=F32)


def pad_lanes(size):
    return (size + 127) // 128 * 128


def one_hot(row, count):
    ids = lax.broadcasted_iota(jnp.int32, (count, row.shape[-1]), 0)
    return ids == row


def as_bf16(mask):
    return jnp.where(mask, 1.0, 0.0).astype(BF)


def load_weights(first, w1_ref, w3_ref, w2_ref, w13, w2p):
    ff = w1_ref.shape[2]
    fp = w2p.shape[0]

    @pl.when(first)
    def _():
        w13[...] = jnp.zeros_like(w13)
        w2p[...] = jnp.zeros_like(w2p)

    w13[:, 0:ff] = w1_ref[0]
    w13[:, fp:fp + ff] = w3_ref[0]
    w2p[0:ff, :] = w2_ref[0]


def fwd_kernel(cap, group, rt_ref, gt_ref, u_ref, w1_ref, w3_ref, w2_ref, y_ref, w13, w2p, xs, go):
    expert = pl.program_id(0)
    sources, tokens, width = u_ref.shape
    fp = w2p.shape[0]
    load_weights(expert == 0, w1_ref, w3_ref, w2_ref, w13, w2p)

    @pl.when(expert == 0)
    def _():
        y_ref[...] = jnp.zeros_like(y_ref)

    slot = lax.rem(expert, group)

    @pl.loop(0, sources)
    def _(s):
        mask = one_hot(rt_ref[expert, s], cap)
        x = jnp.dot(as_bf16(mask), u_ref[s], preferred_element_type=F32).astype(BF)
        gate = jnp.sum(jnp.where(mask, gt_ref[expert, s], 0.0), axis=1, keepdims=True)
        a = jnp.dot(x, w13[...], preferred_element_type=F32)
        a1 = a[:, 0:fp]
        a3 = a[:, fp:2 * fp]
        h = (jax.nn.silu(a1) * a3).astype(BF)
        o = jnp.dot(h, w2p[...], preferred_element_type=F32).astype(BF)
        p = o.astype(F32) * gate
        hi = p.astype(BF)
        rest = p - hi.astype(F32)
        mid = rest.astype(BF)
        low = (rest - mid.astype(F32)).astype(BF)
        rows = pl.ds(pl.multiple_of(slot * cap, 16), cap)
        go[s, rows, 0:width] = hi
        go[s, rows, width:2 * width] = mid
        go[s, rows, 2 * width:3 * width] = low

    @pl.when(slot == group - 1)
    def _():
        tile = 256

        @pl.loop(0, sources * (tokens // tile))
        def _(step):
            s = step // (tokens // tile)
            at = pl.ds(pl.multiple_of(lax.rem(step, tokens // tile) * tile, tile), tile)
            hot = jnp.concatenate([as_bf16(one_hot(rt_ref[expert - (group - 1) + k, s, :, at], cap)) for k in range(group)], axis=0)
            d = contract_rows(hot, go[s])
            y_ref[s, at, :] += d[:, 0:width] + (d[:, width:2 * width] + d[:, 2 * width:3 * width])


def bwd_kernel(cap, count, has_acc, base_ref, rt_ref, gt_ref, u_ref, dy_ref, w1_ref, w3_ref, w2_ref, *rest):
    if has_acc:
        acc_ref, *rest = rest
    g1_ref, g3_ref, g2_ref, du_ref, w13, w2p, xs, ds, hs, das, dxs, hots = rest
    step = pl.program_id(0)
    sources, tokens, width = u_ref.shape
    ff = w1_ref.shape[2]
    fp = w2p.shape[0]

    @pl.when(step < count)
    def _():
        expert = base_ref[0] + step
        load_weights(step == 0, w1_ref, w3_ref, w2_ref, w13, w2p)

        @pl.loop(0, sources)
        def _(s):
            mask = one_hot(rt_ref[expert, s], cap)
            hot = as_bf16(mask)
            gate = jnp.sum(jnp.where(mask, gt_ref[expert, s], 0.0), axis=1, keepdims=True)
            rows = pl.ds(pl.multiple_of(s * cap, 16), cap)
            xs[rows, :] = jnp.dot(hot, u_ref[s], preferred_element_type=F32).astype(BF)
            ds[rows, :] = (jnp.dot(hot, dy_ref[s], preferred_element_type=F32) * gate).astype(BF)

        @pl.loop(0, sources // 2)
        def _(c):
            rows = pl.ds(pl.multiple_of(c * 2 * cap, 16), 2 * cap)
            a = jnp.dot(xs[rows, :], w13[...], preferred_element_type=F32)
            dh = contract_cols(ds[rows, :], w2p[...])
            a1 = a[:, 0:fp]
            a3 = a[:, fp:2 * fp]
            sigma = jax.nn.sigmoid(a1)
            si = a1 * sigma
            hs[rows, :] = (si * a3).astype(BF)
            das[rows, 0:fp] = (dh * a3 * (sigma * (1.0 + a1 * (1.0 - sigma)))).astype(BF)
            das[rows, fp:2 * fp] = (dh * si).astype(BF)
            dx = contract_cols(das[rows, :], w13[...]).astype(BF)
            into = pl.ds(pl.multiple_of(step * cap, 16), cap)
            dxs[2 * c, into, :] = dx[0:cap]
            dxs[2 * c + 1, into, :] = dx[cap:2 * cap]

        g2 = contract_rows(hs[...], ds[...])
        g2_ref[0] = g2[0:ff].astype(BF)
        g1 = contract_rows(xs[...], das[:, 0:fp])
        g1_ref[0] = g1[:, 0:ff].astype(BF)
        g3 = contract_rows(xs[...], das[:, fp:2 * fp])
        g3_ref[0] = g3[:, 0:ff].astype(BF)

    @pl.when(step >= count)
    def _():
        tile = hots.shape[1]
        s = step - count

        @pl.loop(0, tokens // tile)
        def _(t):
            at = pl.ds(pl.multiple_of(t * tile, tile), tile)
            for k in range(count):
                hots[k * cap:(k + 1) * cap, :] = as_bf16(one_hot(rt_ref[base_ref[0] + k, s, :, at], cap))
            d = contract_rows(hots[...], dxs[s])
            if has_acc:
                d = d + acc_ref[0, at, :]
            du_ref[0, at, :] = d.astype(du_ref.dtype)


def full_spec(shape):
    return pl.BlockSpec(shape, lambda *_: (0,) * len(shape), pipeline_mode=pl.Buffered(1))


def experts_forward(rt, gt, u, w_gate, w_up, w_down, cap):
    experts, width, ff = w_gate.shape
    sources, tokens, _ = u.shape
    fp = pad_lanes(ff)
    group = 4
    rows = experts * sources * cap
    spec = lambda a, b: pl.BlockSpec((1, a, b), lambda e: (e, 0, 0))
    return pl.pallas_call(
        functools.partial(fwd_kernel, cap, group),
        out_shape=jax.ShapeDtypeStruct((sources, tokens, width), F32),
        grid=(experts,),
        in_specs=[full_spec(rt.shape), full_spec(gt.shape), full_spec(u.shape), spec(width, ff), spec(width, ff), spec(ff, width)],
        out_specs=full_spec((sources, tokens, width)),
        scratch_shapes=[
            pltpu.VMEM((width, 2 * fp), BF),
            pltpu.VMEM((fp, width), BF),
            pltpu.VMEM((8, 128), BF),
            pltpu.VMEM((sources, group * cap, 3 * width), BF),
        ],
        compiler_params=pltpu.CompilerParams(vmem_limit_bytes=VMEM_LIMIT),
        cost_estimate=pl.CostEstimate(flops=2 * rows * width * (4 * tokens + 3 * ff), bytes_accessed=experts * 3 * width * ff * 2 + u.size * 6, transcendentals=0),
        name="experts_forward",
    )(rt, gt, u, w_gate, w_up, w_down)


def experts_backward(base, count, rt, gt, u, dy, w_gate, w_up, w_down, cap, acc):
    _, width, ff = w_gate.shape
    sources, tokens, _ = u.shape
    fp = pad_lanes(ff)
    has_acc = acc is not None
    rows = count * sources * cap
    last = count - 1
    win = lambda a, b: pl.BlockSpec((1, a, b), lambda i, base_ref: (base_ref[0] + jnp.minimum(i, last), 0, 0))
    wout = lambda a, b: pl.BlockSpec((1, a, b), lambda i, base_ref: (jnp.minimum(i, last), 0, 0))
    part = pl.BlockSpec((1, tokens, width), lambda i, base_ref: (jnp.maximum(i - count, 0), 0, 0))
    in_specs = [full_spec(rt.shape), full_spec(gt.shape), full_spec(u.shape), full_spec(dy.shape), win(width, ff), win(width, ff), win(ff, width)]
    args = [rt, gt, u, dy, w_gate, w_up, w_down]
    if has_acc:
        in_specs.append(part)
        args.append(acc)
    return pl.pallas_call(
        functools.partial(bwd_kernel, cap, count, has_acc),
        out_shape=(
            jax.ShapeDtypeStruct((count, width, ff), BF),
            jax.ShapeDtypeStruct((count, width, ff), BF),
            jax.ShapeDtypeStruct((count, ff, width), BF),
            jax.ShapeDtypeStruct((sources, tokens, width), BF if has_acc else F32),
        ),
        grid_spec=pltpu.PrefetchScalarGridSpec(
            num_scalar_prefetch=1,
            grid=(count + sources,),
            in_specs=in_specs,
            out_specs=(wout(width, ff), wout(width, ff), wout(ff, width), part),
            scratch_shapes=[
                pltpu.VMEM((width, 2 * fp), BF),
                pltpu.VMEM((fp, width), BF),
                pltpu.VMEM((sources * cap, width), BF),
                pltpu.VMEM((sources * cap, width), BF),
                pltpu.VMEM((sources * cap, fp), BF),
                pltpu.VMEM((sources * cap, 2 * fp), BF),
                pltpu.VMEM((sources, count * cap, width), BF),
                pltpu.VMEM((count * cap, 256), BF),
            ],
        ),
        compiler_params=pltpu.CompilerParams(vmem_limit_bytes=VMEM_LIMIT),
        cost_estimate=pl.CostEstimate(flops=2 * rows * width * (3 * tokens + 8 * ff), bytes_accessed=count * 6 * width * ff * 2 + u.size * 6, transcendentals=0),
        name="experts_backward",
    )(base, *args)


def solution(mesh):
    ep_size = mesh.shape["ep"]
    dp_size = mesh.shape["dp"]
    tok_spec = P(ALL_AXES, None)
    route_spec = P(None, ALL_AXES, None)
    exp_spec = P(None, "ep", None, None)
    repl_spec = P(None, None, None)
    core_perm = [(i, i ^ 1) for i in range(dp_size)]
    x_perm = [(i, i ^ 2) for i in range(dp_size)]

    def to_f32(value):
        return value.astype(F32)

    def gather_ep(value):
        return lax.all_gather(value, "ep", axis=0)

    def sum_home(parts):
        back = lax.all_to_all(parts, "ep", 0, 0)
        return jnp.sum(to_f32(back), axis=0)

    def reduce_experts(theirs, mine):
        mine = [(to_f32(m) + to_f32(lax.ppermute(t, "dp", core_perm))).astype(BF) for t, m in zip(theirs, mine)]
        total = [(to_f32(m) + to_f32(lax.ppermute(m, "dp", x_perm))).astype(BF) for m in mine]
        other = [lax.ppermute(t, "dp", core_perm) for t in total]
        return total, other

    def body(act_in, grad_out, slot_ids, gate_vals, w_dense, w_gate, w_up, w_down, ws_gate, ws_up, ws_down):
        layers = w_dense.shape[0]
        tokens, width = act_in.shape
        top = slot_ids.shape[2]
        experts = w_gate.shape[1]
        half = experts // 2
        cap = 2 * tokens * top // (experts * ep_size)
        core = lax.rem(lax.axis_index("dp"), 2)
        first = experts * lax.axis_index("ep")

        meta = jnp.concatenate([slot_ids.astype(F32), gate_vals], axis=2).transpose(0, 2, 1)
        meta = gather_ep(meta)
        slots = meta[:, :, 0:top].astype(jnp.int32).transpose(1, 0, 2, 3)[:, None]
        gates = meta[:, :, top:].transpose(1, 0, 2, 3)[:, None]
        ids = first + lax.broadcasted_iota(jnp.int32, (1, experts, 1, 1, 1), 1)
        match = slots // cap == ids
        rt_all = jnp.max(jnp.where(match, slots % cap, -1), axis=3)[:, :, :, None]
        gt_all = jnp.sum(jnp.where(match, gates, 0.0), axis=3)[:, :, :, None]

        acts = [act_in]
        mixed = []
        mixed_all = []
        grad_out_all = gather_ep(grad_out)
        for layer in range(layers):
            act = acts[layer]
            u = (to_f32(act) + jnp.dot(act, w_dense[layer], preferred_element_type=F32)).astype(BF)
            mixed.append(u)
            mixed_all.append(gather_ep(u))
            if layer + 1 < layers:
                parts = experts_forward(rt_all[layer], gt_all[layer], mixed_all[layer], w_gate[layer], w_up[layer], w_down[layer], cap)
                s_one = jnp.dot(u, ws_gate[layer], preferred_element_type=F32)
                s_three = jnp.dot(u, ws_up[layer], preferred_element_type=F32)
                shared_hidden = (jax.nn.silu(s_one) * s_three).astype(BF)
                shared_out = jnp.dot(shared_hidden, ws_down[layer], preferred_element_type=F32)
                acts.append((to_f32(u) + sum_home(parts) + shared_out).astype(BF))

        grad_y = grad_out
        dense_sums = [None] * layers
        expert_sums = [None] * layers
        for layer in reversed(range(layers)):
            u = mixed[layer]
            grad_all = grad_out_all if layer + 1 == layers else gather_ep(grad_y)
            call = lambda base, acc: experts_backward(
                base.reshape(1), half, rt_all[layer], gt_all[layer], mixed_all[layer], grad_all,
                w_gate[layer], w_up[layer], w_down[layer], cap, acc)
            *theirs, acc = call(half * (1 - core), None)
            *own, parts = call(half * core, acc)
            expert_sums[layer] = reduce_experts(theirs, own)

            s_one = jnp.dot(u, ws_gate[layer], preferred_element_type=F32)
            s_three = jnp.dot(u, ws_up[layer], preferred_element_type=F32)
            shared_hidden = (jax.nn.silu(s_one) * s_three).astype(BF)
            g_ws_down = contract_rows(shared_hidden, grad_y)
            grad_shared = contract_cols(grad_y, ws_down[layer])
            grad_s_one = (grad_shared * s_three * silu_grad(s_one)).astype(BF)
            grad_s_three = (grad_shared * jax.nn.silu(s_one)).astype(BF)
            g_ws_gate = contract_rows(u, grad_s_one)
            g_ws_up = contract_rows(u, grad_s_three)
            grad_mixed = (to_f32(grad_y) + sum_home(parts) + contract_cols(grad_s_one, ws_gate[layer]) + contract_cols(grad_s_three, ws_up[layer])).astype(BF)
            g_w_dense = contract_rows(acts[layer], grad_mixed)
            grad_y = (to_f32(grad_mixed) + contract_cols(grad_mixed, w_dense[layer])).astype(BF)
            dense = tuple(g.astype(BF) for g in (g_w_dense, g_ws_gate, g_ws_up, g_ws_down))
            if layer + 1 < layers:
                dense, later = lax.optimization_barrier((dense, dense_sums[layer + 1]))
                dense_sums[layer + 1] = later
            dense_sums[layer] = tuple(lax.psum(g, ALL_AXES) for g in dense)

        dense_out = [jnp.stack([dense_sums[layer][which] for layer in range(layers)]) for which in range(4)]
        expert_out = []
        for which in range(3):
            total = jnp.stack([expert_sums[layer][0][which] for layer in range(layers)])
            other = jnp.stack([expert_sums[layer][1][which] for layer in range(layers)])
            expert_out.append(jnp.where(core == 0, jnp.concatenate([total, other], axis=1), jnp.concatenate([other, total], axis=1)))
        return (grad_y, dense_out[0], expert_out[0], expert_out[1], expert_out[2], dense_out[1], dense_out[2], dense_out[3])

    return jax.shard_map(body, mesh=mesh, in_specs=(tok_spec, tok_spec, route_spec, route_spec, repl_spec, exp_spec, exp_spec, exp_spec, repl_spec, repl_spec, repl_spec), out_specs=(tok_spec, repl_spec, exp_spec, exp_spec, exp_spec, repl_spec, repl_spec, repl_spec), check_vma=False)
```

time: 2290 us -> 1200 us (0.52)
  waiting for transfers between devices: 1080 us -> 370 us
  Pallas kernels: 0 us -> 378 us
  local copies, waits for them, and re-layouts: 539 us -> 216 us
  matrix products: 339 us -> 53.7 us
  blocking collectives: 143 us -> 13.7 us
    psum x2, waiting for transfers between devices: 624 us -> 67.6 us  [body(): dense_sums[layer] = tuple((lax.psum(g, ALL_AXES) for g in dense))]
    pallas_call x0 -> x5, Pallas kernels: none -> 378 us  [the longest x4 256 us: experts_backward(): pl.pallas_call(functools.partial(bwd_kernel, cap, count, has_acc), out_sh...]
    all_to_all x6 -> x3, waiting for transfers between devices: 455 us -> 151 us  [sum_home(): back = lax.all_to_all(parts, 'ep', 0, 0)]
    gather x7 -> x0, local copies, waits for them, and re-layouts: 304 us -> none  [the longest x2 108 us: layer_backward(): jnp.take(grad_ext, slot_owner, axis=0)]
    dot_general x24 -> x7, matrix products: 306 us -> 15.5 us  [the longest x2 5.06 us: body(): jnp.dot(act, w_dense[layer], preferred_element_type=F32)]
    all_to_all x1 -> x0, blocking collectives: 143 us -> none  [layer_front(): lax.all_to_all(send_buf, 'ep', 0, 1)]
    ppermute x0 -> x18, waiting for transfers between devices: none -> 121 us  [the longest x6 121 us: reduce_experts(): lax.ppermute(m, 'dp', x_perm)]
    unnamed x123 -> x98, local copies, waits for them, and re-layouts: 13.1 us -> 84.1 us
  transfers between devices with their start and end apart: 8 -> 27, of which waited for: 8 -> 7; matrix products, arithmetic and copies ran while one was open for 17% -> 29% of each run, Pallas kernels for 0% -> 11%
where the time goes in v1:
time: 1200 us; the launch traced here: 1190 us
  Pallas kernels  378 us (32%)
  waiting for transfers between devices  370 us (31%)
  local copies, waits for them, and re-layouts  216 us (18%)
  other arithmetic  114 us (10%)
  matrix products  53.7 us (4%)
  starting transfers between devices  25.4 us (2%)
  between operations  14.9 us (1%)
  blocking collectives  13.7 us (1%)
    pallas_call x4, Pallas kernels, experts_backward(): pl.pallas_call(functools.partial(bwd_kernel, cap, count, has_acc), out_sh...  256 us
    all_to_all x3, waiting for transfers between devices, sum_home(): back = lax.all_to_all(parts, 'ep', 0, 0)  151 us
    pallas_call x1, Pallas kernels, experts_forward(): pl.pallas_call(functools.partial(fwd_kernel, cap, group), out_shape=jax.S...  122 us
    ppermute x6, waiting for transfers between devices, reduce_experts(): lax.ppermute(m, 'dp', x_perm)  121 us
    unnamed x98, local copies, waits for them, and re-layouts  84.1 us
    psum x2, waiting for transfers between devices, body(): dense_sums[layer] = tuple((lax.psum(g, ALL_AXES) for g in dense))  67.6 us
    select_n x2, other arithmetic, body(): jnp.where(core == 0, jnp.concatenate([total, other], axis=1), jnp.concate...  36.8 us
    all_gather x4, waiting for transfers between devices, gather_ep(): return lax.all_gather(value, 'ep', axis=0)  30.1 us
  transfers between devices with their start and end apart: 27, of which 7 were waited for; matrix products, arithmetic and copies ran while one was open for 29% of the time, Pallas kernels for 11%

profile of v1, /device:TPU:0, one launch (start us, length us, event | category | flops | bytes accessed | tf_op | source)
XLA Modules:
  0.0 1185.3 jit_solution(1503031056748559336)
XLA Ops:
  10.8 13.7 %all-gather = f32[8,12,1024]{2,1,0:T(8,128)S(1)} all-gather(f32[2,12,1024]{2,1,0:T(8,128)S(1)} %maximum_bitcast_fusion), channel_id=2, replica_groups=mesh['ep'=4,'dp'=4] {'ep'}, dimensions={0}, use_global_device_ids=true | all-gather | bytes 491520 | tf_op jit(solution)/shard_map/all_gather | solution.py:252
  28.1 10.0 fusion.52
  38.1 8.4 copy.113
  46.5 10.0 fusion.51
  56.4 8.4 copy.114
  64.8 9.7 slice_bitcast_fusion
  74.5 122.2 %experts_forward.1 = f32[4,1024,512]{2,1,0:T(8,128)} custom-call(s32[16,4,1,1024]{3,2,1,0:T(1,128)} %bitcast.177, f32[16,4,1,1024]{3,2,1,0:T(1,128)} %bitcast.180, bf16[4,1024,512]{2,1,0:T(8,128)(2,1)} %bitcast.187, bf16[16,512,352]{2,1,0:T(8,128)(2,1)} %bitcast.156, bf16[16,512,352]{2,1,0:T(8,128)(2,1)} %bitcast.159, ...), custom_call_target="tpu_custom_call" | custom-call | flops 64827162624 | bytes 29884416 | tf_op jit(solution)/shard_map/experts_forward/pallas_call | solution.py:175
  210.6 114.2 %all-to-all-done = f32[4,1024,512]{2,1,0:T(8,128)} async-done(((f32[4,1024,512]{2,1,0:T(8,128)}), f32[4,1024,512]{2,1,0:T(8,128)}, u32[]{:S(2)}, u32[]{:S(2)}) %all-to-all-start) | async-done | bytes 8388640 | tf_op jit(solution)/shard_map/all_to_all | solution.py:255
  338.7 8.3 copy.115
  347.1 8.3 copy.116
  355.4 30.1 %all-gather.12.cloned.1.call-done = bf16[4096,512]{1,0:T(8,128)(2,1)} async-done(((bf16[1024,512]{1,0:T(8,128)(2,1)}), bf16[4096,512]{1,0:T(8,128)(2,1)}) %all-gather.12.cloned.1.call-update) | async-done | bytes 4194320 | tf_op jit(solution)/shard_map/all_gather | solution.py:252
  385.5 63.7 %experts_backward.4 = (bf16[8,512,352]{2,1,0:T(8,128)(2,1)}, bf16[8,512,352]{2,1,0:T(8,128)(2,1)}, bf16[8,352,512]{2,1,0:T(8,128)(2,1)}, f32[4,1024,512]{2,1,0:T(8,128)}) custom-call(s32[1]{0:T(128)} %bitcast.25.base_ref, s32[16,4,1,1024]{3,2,1,0:T(1,128)} %bitcast.183, f32[16,4,1,1024]{3,2,1,0:T(1,128)} %bitcast.185, bf16[4,1024,512]{2,1,0:T(8,128)(2,1)} %bitcast.194, ...), custom_call_target="tpu_custom_call" | custom-call | flops 37044092928 | bytes 29884416 | tf_op jit(solution)/shard_map/experts_backward/pallas_call | solution.py:208
  449.2 64.2 %experts_backward.5 = (bf16[8,512,352]{2,1,0:T(8,128)(2,1)}, bf16[8,512,352]{2,1,0:T(8,128)(2,1)}, bf16[8,352,512]{2,1,0:T(8,128)(2,1)}, bf16[4,1024,512]{2,1,0:T(8,128)(2,1)}) custom-call(s32[1]{0:T(128)} %bitcast.base_ref, s32[16,4,1,1024]{3,2,1,0:T(1,128)} %bitcast.184, f32[16,4,1,1024]{3,2,1,0:T(1,128)} %bitcast.186, bf16[4,1024,512]{2,1,0:T(8,128)(2,1)} %bitcast.195, ...), custom_call_target="tpu_custom_call" | custom-call | flops 37044092928 | bytes 29884416 | tf_op jit(solution)/shard_map/experts_backward/pallas_call | solution.py:208
  529.1 36.3 %all-to-all-done.1 = bf16[4,1024,512]{2,1,0:T(8,128)(2,1)} async-done(((bf16[4,1024,512]{2,1,0:T(8,128)(2,1)}), bf16[4,1024,512]{2,1,0:T(8,128)(2,1)}, u32[]{:S(2)}, u32[]{:S(2)}) %all-to-all-start.1) | async-done | bytes 4194336 | tf_op jit(solution)/shard_map/all_to_all | solution.py:255
  628.6 64.1 %experts_backward.6 = (bf16[8,512,352]{2,1,0:T(8,128)(2,1)}, bf16[8,512,352]{2,1,0:T(8,128)(2,1)}, bf16[8,352,512]{2,1,0:T(8,128)(2,1)}, f32[4,1024,512]{2,1,0:T(8,128)}) custom-call(s32[1]{0:T(128)} %bitcast.25.base_ref, s32[16,4,1,1024]{3,2,1,0:T(1,128)} %bitcast.178, f32[16,4,1,1024]{3,2,1,0:T(1,128)} %bitcast.181, bf16[4,1024,512]{2,1,0:T(8,128)(2,1)} %bitcast.188, ...), custom_call_target="tpu_custom_call" | custom-call | flops 37044092928 | bytes 29884416 | tf_op jit(solution)/shard_map/experts_backward/pallas_call | solution.py:208
  700.9 64.2 %experts_backward.7 = (bf16[8,512,352]{2,1,0:T(8,128)(2,1)}, bf16[8,512,352]{2,1,0:T(8,128)(2,1)}, bf16[8,352,512]{2,1,0:T(8,128)(2,1)}, bf16[4,1024,512]{2,1,0:T(8,128)(2,1)}) custom-call(s32[1]{0:T(128)} %bitcast.base_ref, s32[16,4,1,1024]{3,2,1,0:T(1,128)} %bitcast.179, f32[16,4,1,1024]{3,2,1,0:T(1,128)} %bitcast.182, bf16[4,1024,512]{2,1,0:T(8,128)(2,1)} %bitcast.189, ...), custom_call_target="tpu_custom_call" | custom-call | flops 37044092928 | bytes 29884416 | tf_op jit(solution)/shard_map/experts_backward/pallas_call | solution.py:208
  841.1 18.0 %collective-permute-done.7 = bf16[8,512,352]{1,2,0:T(8,128)(2,1)} collective-permute-done((bf16[8,512,352]{1,2,0:T(8,128)(2,1)}, bf16[8,512,352]{1,2,0:T(8,128)(2,1)}, u32[]{:S(2)}, u32[]{:S(2)}) %collective-permute-start.7) | collective-permute-done | bytes 2883616 | tf_op jit(solution)/shard_map/ppermute | solution.py:260
  874.9 55.7 %collective-permute-done.1 = bf16[8,512,352]{1,2,0:T(8,128)(2,1)} collective-permute-done((bf16[8,512,352]{1,2,0:T(8,128)(2,1)}, bf16[8,512,352]{1,2,0:T(8,128)(2,1)}, u32[]{:S(2)}, u32[]{:S(2)}) %collective-permute-start.1) | collective-permute-done | bytes 2883616 | tf_op jit(solution)/shard_map/ppermute | solution.py:260
  945.0 47.4 %collective-permute-done.15 = bf16[8,352,512]{2,1,0:T(8,128)(2,1)} collective-permute-done((bf16[8,352,512]{2,1,0:T(8,128)(2,1)}, bf16[8,352,512]{2,1,0:T(8,128)(2,1)}, u32[]{:S(2)}, u32[]{:S(2)}) %collective-permute-start.15) | collective-permute-done | bytes 2883616 | tf_op jit(solution)/shard_map/ppermute | solution.py:260
  1017.6 67.6 %all-reduce.5.cloned.1.call-done = (bf16[1,512,512]{1,2,0:T(8,128)(2,1)}, bf16[1,512,704]{1,2,0:T(8,128)(2,1)}, bf16[1,512,704]{1,2,0:T(8,128)(2,1)}, bf16[1,704,512]{2,1,0:T(8,128)(2,1)}) async-done(((bf16[1,512,512]{1,2,0:T(8,128)(2,1)}, bf16[1,512,704]{1,2,0:T(8,128)(2,1)}, bf16[1,512,704]{1,2,0:T(8,128)(2,1)}, bf16[1,704,512]{2,1,0:T(8,128)(2,1)}), (bf16[1,512,512]{1,2,0:T(8,128)(2,1)}, ...) | async-done | bytes 2686992 | tf_op jit(solution)/shard_map/psum | solution.py:329
  1108.9 23.8 %maximum_select_fusion = (bf16[2,16,512,352]{3,2,1,0:T(8,128)(2,1)}, bf16[2,16,512,352]{3,2,1,0:T(8,128)(2,1)}) fusion(bf16[1,8,512,352]{3,2,1,0:T(8,128)(2,1)} %bitcast.153, bf16[1,8,512,352]{3,2,1,0:T(8,128)(2,1)} %bitcast.155, bf16[1,8,512,352]{3,2,1,0:T(8,128)(2,1)} %bitcast.149, bf16[1,8,512,352]{3,2,1,0:T(8,128)(2,1)} %bitcast.151, pred[]{:T(512)S(6)} %eq.23, ...), kind=kLoop, calls=%fused_computation | loop fusion | flops 80740352 | bytes 46137344 | tf_op jit(solution)/shard_map/jit(_where)/select_n | solution.py:336
  1132.7 16.2 %copy.106 = bf16[2,16,512,352]{2,3,1,0:T(8,128)(2,1)} copy(bf16[2,16,512,352]{3,2,1,0:T(8,128)(2,1)} %get-tuple-element.108) | data formatting | bytes 23068672
  1149.0 16.2 %copy.107 = bf16[2,16,512,352]{2,3,1,0:T(8,128)(2,1)} copy(bf16[2,16,512,352]{3,2,1,0:T(8,128)(2,1)} %get-tuple-element.109) | data formatting | bytes 23068672
  1165.2 13.0 %maximum_select_fusion.2 = bf16[2,16,352,512]{3,2,1,0:T(8,128)(2,1)} fusion(bf16[1,8,352,512]{3,2,1,0:T(8,128)(2,1)} %bitcast.44, bf16[1,8,352,512]{3,2,1,0:T(8,128)(2,1)} %bitcast.43, bf16[1,8,352,512]{3,2,1,0:T(8,128)(2,1)} %bitcast.42, bf16[1,8,352,512]{3,2,1,0:T(8,128)(2,1)} %bitcast.41, pred[]{:T(512)S(6)} %eq.23), kind=kLoop, calls=%fused_computation.2 | loop fusion | flops 40370176 | bytes 23068672 | tf_op jit(solution)/shard_map/jit(_where)/select_n | solution.py:336
  (218 shorter events, 276.8 us)
Async XLA Ops:
  7.2 67.3 %all-gather.10.cloned.1.call-start = ((), (), s32[]{:S(2)}) async-start(), calls=%async_computation.3 | async-start | bytes 5242880 | tf_op jit(solution)/shard_map/all_gather | solution.py:252
  196.7 128.0 %all-to-all-start = ((f32[4,1024,512]{2,1,0:T(8,128)}), f32[4,1024,512]{2,1,0:T(8,128)}, u32[]{:S(2)}, u32[]{:S(2)}) async-start(f32[4,1024,512]{2,1,0:T(8,128)} %experts_forward.1), calls=%async_computation | async-start | bytes 16777216 | tf_op jit(solution)/shard_map/all_to_all | solution.py:255
  202.5 152.9 %all-gather.14.cloned.1.call-start = ((), (), s32[]{:S(2)}) async-start(), calls=%async_computation.5 | async-start | bytes 5242880 | tf_op jit(solution)/shard_map/all_gather | solution.py:252
  203.2 182.2 %all-gather.12.cloned.1.call-start = ((), (), s32[]{:S(2)}) async-start(), calls=%async_computation.4 | async-start | bytes 5242880 | tf_op jit(solution)/shard_map/all_gather | solution.py:252
  513.3 52.1 %all-to-all-start.1 = ((bf16[4,1024,512]{2,1,0:T(8,128)(2,1)}), bf16[4,1024,512]{2,1,0:T(8,128)(2,1)}, u32[]{:S(2)}, u32[]{:S(2)}) async-start(bf16[4,1024,512]{2,1,0:T(8,128)(2,1)} %get-tuple-element.33), calls=%async_computation.1 | async-start | bytes 8388608 | tf_op jit(solution)/shard_map/all_to_all | solution.py:255
  518.3 110.3 %all-gather.16.cloned.1.call-start = ((), (), s32[]{:S(2)}) async-start(), calls=%async_computation.6 | async-start | bytes 5242880 | tf_op jit(solution)/shard_map/all_gather | solution.py:252
  600.4 201.7 %collective-permute-start.9 = (bf16[8,512,352]{1,2,0:T(8,128)(2,1)}, bf16[8,512,352]{1,2,0:T(8,128)(2,1)}, u32[]{:S(2)}, u32[]{:S(2)}) collective-permute-start(bf16[8,512,352]{1,2,0:T(8,128)(2,1)} %copy.99), channel_id=1, source_target_pairs={{0,2},{1,3},{2,0},{3,1},{4,6},{5,7},{6,4},{7,5},{8,10},{9,11},{10,... | collective-permute-start | bytes 8650760 | tf_op jit(solution)/shard_map/ppermute | solution.py:260
  613.4 203.1 %collective-permute-start.3 = (bf16[8,512,352]{1,2,0:T(8,128)(2,1)}, bf16[8,512,352]{1,2,0:T(8,128)(2,1)}, u32[]{:S(2)}, u32[]{:S(2)}) collective-permute-start(bf16[8,512,352]{1,2,0:T(8,128)(2,1)} %copy.87), channel_id=1, source_target_pairs={{0,2},{1,3},{2,0},{3,1},{4,6},{5,7},{6,4},{7,5},{8,10},{9,11},{10,... | collective-permute-start | bytes 8650760 | tf_op jit(solution)/shard_map/ppermute | solution.py:260
  692.7 138.4 %collective-permute-start.12 = (bf16[8,352,512]{2,1,0:T(8,128)(2,1)}, bf16[8,352,512]{2,1,0:T(8,128)(2,1)}, u32[]{:S(2)}, u32[]{:S(2)}) collective-permute-start(bf16[8,352,512]{2,1,0:T(8,128)(2,1)} %get-tuple-element.47), channel_id=1, source_target_pairs={{0,1},{1,0},{2,3},{3,2},{4,5},{5,4},{6,7},{7,6},{8,9},{9,8},{10,11... | collective-permute-start | bytes 8650760 | tf_op jit(solution)/shard_map/ppermute | solution.py:259
  697.5 72.5 %collective-permute-start.6 = (bf16[8,512,352]{1,2,0:T(8,128)(2,1)}, bf16[8,512,352]{1,2,0:T(8,128)(2,1)}, u32[]{:S(2)}, u32[]{:S(2)}) collective-permute-start(bf16[8,512,352]{1,2,0:T(8,128)(2,1)} %copy.93), channel_id=1, source_target_pairs={{0,1},{1,0},{2,3},{3,2},{4,5},{5,4},{6,7},{7,6},{8,9},{9,8},{10,11... | collective-permute-start | bytes 8650760 | tf_op jit(solution)/shard_map/ppermute | solution.py:259
  700.8 82.1 %collective-permute-start = (bf16[8,512,352]{1,2,0:T(8,128)(2,1)}, bf16[8,512,352]{1,2,0:T(8,128)(2,1)}, u32[]{:S(2)}, u32[]{:S(2)}) collective-permute-start(bf16[8,512,352]{1,2,0:T(8,128)(2,1)} %copy.81), channel_id=1, source_target_pairs={{0,1},{1,0},{2,3},{3,2},{4,5},{5,4},{6,7},{7,6},{8,9},{9,8},{10,11... | collective-permute-start | bytes 8650760 | tf_op jit(solution)/shard_map/ppermute | solution.py:259
  765.1 71.7 %all-to-all-start.2 = ((bf16[4,1024,512]{2,1,0:T(8,128)(2,1)}), bf16[4,1024,512]{2,1,0:T(8,128)(2,1)}, u32[]{:S(2)}, u32[]{:S(2)}) async-start(bf16[4,1024,512]{2,1,0:T(8,128)(2,1)} %get-tuple-element.35), calls=%async_computation.2 | async-start | bytes 8388608 | tf_op jit(solution)/shard_map/all_to_all | solution.py:255
  769.9 229.1 %all-reduce.7.cloned.1.call-start = ((), (), s32[]{:S(2)}) async-start(), calls=%async_computation.8 | async-start | bytes 5373952 | tf_op jit(solution)/shard_map/psum | solution.py:329
  781.4 77.6 %collective-permute-start.7 = (bf16[8,512,352]{1,2,0:T(8,128)(2,1)}, bf16[8,512,352]{1,2,0:T(8,128)(2,1)}, u32[]{:S(2)}, u32[]{:S(2)}) collective-permute-start(bf16[8,512,352]{1,2,0:T(8,128)(2,1)} %copy.95), channel_id=1, source_target_pairs={{0,2},{1,3},{2,0},{3,1},{4,6},{5,7},{6,4},{7,5},{8,10},{9,11},{10,... | collective-permute-start | bytes 8650760 | tf_op jit(solution)/shard_map/ppermute | solution.py:260
  794.4 136.2 %collective-permute-start.1 = (bf16[8,512,352]{1,2,0:T(8,128)(2,1)}, bf16[8,512,352]{1,2,0:T(8,128)(2,1)}, u32[]{:S(2)}, u32[]{:S(2)}) collective-permute-start(bf16[8,512,352]{1,2,0:T(8,128)(2,1)} %copy.83), channel_id=1, source_target_pairs={{0,2},{1,3},{2,0},{3,1},{4,6},{5,7},{6,4},{7,5},{8,10},{9,11},{10,... | collective-permute-start | bytes 8650760 | tf_op jit(solution)/shard_map/ppermute | solution.py:260
  798.2 287.0 %all-reduce.5.cloned.1.call-start = ((), (), s32[]{:S(2)}) async-start(), calls=%async_computation.7 | async-start | bytes 5373952 | tf_op jit(solution)/shard_map/psum | solution.py:329
  802.1 190.3 %collective-permute-start.15 = (bf16[8,352,512]{2,1,0:T(8,128)(2,1)}, bf16[8,352,512]{2,1,0:T(8,128)(2,1)}, u32[]{:S(2)}, u32[]{:S(2)}) collective-permute-start(bf16[8,352,512]{2,1,0:T(8,128)(2,1)} %add_convert_fusion.9), channel_id=1, source_target_pairs={{0,2},{1,3},{2,0},{3,1},{4,6},{5,7},{6,4},{7,5},{8,10},{9,11},{10,... | collective-permute-start | bytes 8650760 | tf_op jit(solution)/shard_map/ppermute | solution.py:260
  816.6 187.7 %collective-permute-start.11 = (bf16[8,512,352]{1,2,0:T(8,128)(2,1)}, bf16[8,512,352]{1,2,0:T(8,128)(2,1)}, u32[]{:S(2)}, u32[]{:S(2)}) collective-permute-start(bf16[8,512,352]{1,2,0:T(8,128)(2,1)} %copy.103), channel_id=1, source_target_pairs={{0,1},{1,0},{2,3},{3,2},{4,5},{5,4},{6,7},{7,6},{8,9},{9,8},{10,11... | collective-permute-start | bytes 8650760 | tf_op jit(solution)/shard_map/ppermute | solution.py:261
  831.1 178.4 %collective-permute-start.5 = (bf16[8,512,352]{1,2,0:T(8,128)(2,1)}, bf16[8,512,352]{1,2,0:T(8,128)(2,1)}, u32[]{:S(2)}, u32[]{:S(2)}) collective-permute-start(bf16[8,512,352]{1,2,0:T(8,128)(2,1)} %copy.91), channel_id=1, source_target_pairs={{0,1},{1,0},{2,3},{3,2},{4,5},{5,4},{6,7},{7,6},{8,9},{9,8},{10,11... | collective-permute-start | bytes 8650760 | tf_op jit(solution)/shard_map/ppermute | solution.py:261
  859.1 235.4 %collective-permute-start.13 = (bf16[8,352,512]{2,1,0:T(8,128)(2,1)}, bf16[8,352,512]{2,1,0:T(8,128)(2,1)}, u32[]{:S(2)}, u32[]{:S(2)}) collective-permute-start(bf16[8,352,512]{2,1,0:T(8,128)(2,1)} %add_convert_fusion.11), channel_id=1, source_target_pairs={{0,2},{1,3},{2,0},{3,1},{4,6},{5,7},{6,4},{7,5},{8,10},{9,11},{10,... | collective-permute-start | bytes 8650760 | tf_op jit(solution)/shard_map/ppermute | solution.py:260
  930.6 169.1 %collective-permute-start.10 = (bf16[8,512,352]{1,2,0:T(8,128)(2,1)}, bf16[8,512,352]{1,2,0:T(8,128)(2,1)}, u32[]{:S(2)}, u32[]{:S(2)}) collective-permute-start(bf16[8,512,352]{1,2,0:T(8,128)(2,1)} %copy.101), channel_id=1, source_target_pairs={{0,1},{1,0},{2,3},{3,2},{4,5},{5,4},{6,7},{7,6},{8,9},{9,8},{10,11... | collective-permute-start | bytes 8650760 | tf_op jit(solution)/shard_map/ppermute | solution.py:261
  992.4 111.9 %collective-permute-start.4 = (bf16[8,512,352]{1,2,0:T(8,128)(2,1)}, bf16[8,512,352]{1,2,0:T(8,128)(2,1)}, u32[]{:S(2)}, u32[]{:S(2)}) collective-permute-start(bf16[8,512,352]{1,2,0:T(8,128)(2,1)} %copy.89), channel_id=1, source_target_pairs={{0,1},{1,0},{2,3},{3,2},{4,5},{5,4},{6,7},{7,6},{8,9},{9,8},{10,11... | collective-permute-start | bytes 8650760 | tf_op jit(solution)/shard_map/ppermute | solution.py:261
  1004.3 161.0 %collective-permute-start.17 = (bf16[8,352,512]{2,1,0:T(8,128)(2,1)}, bf16[8,352,512]{2,1,0:T(8,128)(2,1)}, u32[]{:S(2)}, u32[]{:S(2)}) collective-permute-start(bf16[8,352,512]{2,1,0:T(8,128)(2,1)} %add_convert_fusion.8), channel_id=1, source_target_pairs={{0,1},{1,0},{2,3},{3,2},{4,5},{5,4},{6,7},{7,6},{8,9},{9,8},{10,11... | collective-permute-start | bytes 8650760 | tf_op jit(solution)/shard_map/ppermute | solution.py:261
  1099.7 65.6 %collective-permute-start.16 = (bf16[8,352,512]{2,1,0:T(8,128)(2,1)}, bf16[8,352,512]{2,1,0:T(8,128)(2,1)}, u32[]{:S(2)}, u32[]{:S(2)}) collective-permute-start(bf16[8,352,512]{2,1,0:T(8,128)(2,1)} %add_convert_fusion.10), channel_id=1, source_target_pairs={{0,1},{1,0},{2,3},{3,2},{4,5},{5,4},{6,7},{7,6},{8,9},{9,8},{10,11... | collective-permute-start | bytes 8650760 | tf_op jit(solution)/shard_map/ppermute | solution.py:261
  (46 other events, 247.3 us)
Sparse Core Ops, SparseCore 0:
  10.8 51.3 all-gather.9
  205.1 114.6 all-gather.13
  336.9 48.5 all-gather.11
  572.8 48.6 all-gather.15
  798.3 94.0 all-reduce.6
  999.2 85.9 all-reduce.4
